TPU v7x, 32 devices: a whole 2x2x4 slice. The times are simulated.
32 devices in a mesh: groups: 2 (over y), expert: 8 (over z, x), sub: 2 (over core).
Axes of the slice: x: 2, y: 2, z: 4, core: 2. Of those that a mesh axis runs over, the one named last changes fastest.
Arguments:
- stream_in: bfloat16 [1024, 3072], P(('groups', 'expert'), 'sub'), parts along dimension 0, may hold values from -0.29882812 to 0.29882812
- queries: bfloat16 [1024, 3072], P(('groups', 'expert'), 'sub'), parts along dimension 0, may hold values from -6 to 6
- kv_new: bfloat16 [2, 1024, 1024], P(None, ('groups', 'expert'), 'sub'), parts along dimension 1, may hold values from -6 to 6
- paged_key_value_cache: bfloat16 [2, 32, 4, 1024], P(None, ('groups', 'expert'), None, 'sub'), parts along dimension 1, may hold values from -6 to 6
- page_table: int32 [16, 8], P(('groups', 'expert')), parts along dimension 0, may hold values from 0 to 15, as said below
- prefix_len: int32 [16], P(('groups', 'expert')), parts along dimension 0, may hold values from 8 to 32
- norm_gain: float32 [3072], replicated, may hold values from 0.5 to 1.5
- w_router: bfloat16 [3072, 8], replicated, may hold values from -0.21875 to 0.21875
- expert_ids: int32 [1024, 2], P(('groups', 'expert')), parts along dimension 0, may hold values from 0 to 7, as said below
- w_in: bfloat16 [2, 3072, 65536], P(None, None, ('expert', 'sub')), may hold values from -0.109375 to 0.109375
Outputs:
- stream: bfloat16 [1024, 3072], P(('groups', 'expert'), 'sub'), parts along dimension 0
- expert_hidden: bfloat16 [272, 65536], P('groups', ('expert', 'sub')), parts along dimension 0
There are 2 independent parts, one for each index of `groups`. A program takes and returns all parts, laid end to end along the dimension named above; an argument that names none is the same for every part. Nothing has to cross between parts.
Inputs may be any that keep to these rules, and one draw needn't show every extreme that they name: `expert_ids`: each row names two different experts. The rows of one request name each expert at most 17 times, and one expert is named exactly 17 times by the rows of every request. `page_table`: the pages of one row lie in different shards: page // 2 differs along a row. Requests share leading pages.
All inputs are finite; a program needn't handle non-finite values.
Results may differ from a plain program's by a relative error of at most 0.018.
Values may be sent and summed in bfloat16 or wider, within the bound.
A program may use at most 128 MiB of HBM per device.

v0:
```python
import math
import jax
import jax.numpy as jnp
from jax import lax
from jax.sharding import PartitionSpec as P

HEAD_WIDTH = 128
EXPERTS = 8
TOP = 2
CAP = 17


def for_sending(array):

    def short(part):
        return part.astype(jnp.bfloat16) if part.dtype == jnp.float32 else part

    return jax.tree.map(short, array)


def partner(array, axis, apart):
    return lax.ppermute(array, axis, [(i, i ^ 1 << apart) for i in range(lax.axis_size(axis))])


def from_behind(value, axis, steps):
    count = lax.axis_size(axis)
    pairs = [(source, (source + steps) % count) for source in range(count)]
    return lax.ppermute(value, axis, pairs)


def attend(query_rows, key_rows, prefix_length, head_size):
    tokens_here = query_rows.shape[0]
    length = key_rows.shape[1]
    kv_heads = key_rows.shape[2] // head_size
    grouped = query_rows.shape[1] // head_size // kv_heads
    query_f = query_rows.reshape(tokens_here, kv_heads, grouped, head_size).astype(jnp.float32)
    keys_f = key_rows[0].reshape(length, kv_heads, head_size).astype(jnp.float32)
    values_f = key_rows[1].reshape(length, kv_heads, head_size).astype(jnp.float32)
    scores = jnp.einsum("tkgd,lkd->kgtl", query_f, keys_f) * (1.0 / math.sqrt(head_size))
    prefix_span = length - tokens_here
    places = jnp.arange(length)[None, :]
    rows_at = jnp.arange(tokens_here)[:, None]
    is_live = jnp.where(
        places < prefix_span, places < prefix_length, places - prefix_span <= rows_at
    )
    scores = jnp.where(is_live, scores, -1e30)
    largest = jnp.max(scores, axis=-1, keepdims=True)
    exponent = jnp.exp(scores - largest)
    weights = (exponent / jnp.sum(exponent, axis=-1, keepdims=True)).astype(jnp.bfloat16)
    mixed_heads = jnp.einsum("kgtl,lkd->tkgd", weights.astype(jnp.float32), values_f)
    return mixed_heads.reshape(tokens_here, -1).astype(jnp.bfloat16)


def pick_block(stack_rows, position):
    return lax.dynamic_index_in_dim(stack_rows, position, 0, keepdims=False)


def spread(kept_rows, kept_shares, own_index, level_values):
    for depth_bit in range(level_values):
        partner_rows, partner_shares = (
            partner(for_sending(kept_rows), "expert", depth_bit).astype(kept_rows.dtype),
            partner(for_sending(kept_shares), "expert", depth_bit).astype(kept_shares.dtype),
        )
        high_bit = (own_index >> depth_bit) % 2 == 1
        lower_rows = jnp.where(high_bit, partner_rows, kept_rows)
        upper_rows = jnp.where(high_bit, kept_rows, partner_rows)
        lower_shares = jnp.where(high_bit, partner_shares, kept_shares)
        upper_shares = jnp.where(high_bit, kept_shares, partner_shares)
        kept_rows = jnp.concatenate([lower_rows, upper_rows], axis=0)
        kept_shares = jnp.concatenate([lower_shares, upper_shares], axis=0)
    return (kept_rows, kept_shares)


def shards(
    stream_in,
    queries,
    kv_new,
    paged_key_value_cache,
    page_table,
    prefix_len,
    norm_gain,
    w_router,
    expert_ids,
    w_in,
):
    expert_count = lax.axis_size("expert")
    group_width = expert_count // EXPERTS
    level_values = group_width.bit_length() - 1
    own_index = lax.axis_index("expert")
    own_group = own_index // group_width
    shard_pages = paged_key_value_cache.shape[1]
    page_list = page_table[0]
    owners = page_list // shard_pages
    inside = page_list % shard_pages
    owner_hot = owners[None, :] == jnp.arange(expert_count, dtype=jnp.int32)[:, None]
    wanted = jnp.sum(jnp.where(owner_hot, inside[None, :], 0), axis=1)
    asked_for = lax.all_to_all(wanted[:, None], "expert", split_axis=0, concat_axis=0, tiled=True)
    served = jnp.take(paged_key_value_cache, asked_for[:, 0], axis=1)
    arrived = lax.all_to_all(served, "expert", split_axis=1, concat_axis=1, tiled=True)
    prefix_pages = jnp.take(arrived, owners, axis=1)
    prefix_row_block = prefix_pages.reshape(2, -1, prefix_pages.shape[-1])
    key_rows = jnp.concatenate([prefix_row_block, kv_new], axis=1)
    attended = attend(queries, key_rows, prefix_len[0], HEAD_WIDTH)
    stream_part = (stream_in.astype(jnp.float32) + attended.astype(jnp.float32)).astype(
        jnp.bfloat16
    )
    stream = lax.all_gather(stream_part, "sub", axis=1, tiled=True)
    stream_f = stream.astype(jnp.float32)
    scale_rows = lax.rsqrt(jnp.mean(stream_f * stream_f, axis=-1, keepdims=True) + 1e-05)
    normed = (stream_f * scale_rows * norm_gain).astype(jnp.bfloat16)
    logits = jnp.dot(normed, w_router, preferred_element_type=jnp.float32)
    chosen = jnp.take_along_axis(logits, expert_ids, axis=1)
    gate_share = jax.nn.sigmoid(chosen - chosen[:, ::-1])
    row_count = stream_in.shape[0]
    routes = expert_ids.reshape(-1)
    route_count = routes.shape[0]
    expert_hot = (routes[:, None] == jnp.arange(EXPERTS, dtype=jnp.int32)[None, :]).astype(
        jnp.int32
    )
    route_rank = jnp.sum((jnp.cumsum(expert_hot, axis=0) - 1) * expert_hot, axis=1)
    slot_hot = (route_rank[:, None] == jnp.arange(CAP, dtype=jnp.int32)[None, :]).astype(
        jnp.float32
    )
    row_hot = ((jnp.arange(route_count) // TOP)[:, None] == jnp.arange(row_count)[None, :]).astype(
        jnp.float32
    )
    route_place = expert_hot.astype(jnp.float32)[:, :, None] * slot_hot[:, None, :]
    picker = jnp.einsum("rem,rt->emt", route_place, row_hot)
    shares = jnp.einsum("rem,r->em", route_place, gate_share.reshape(-1))
    outgoing = jnp.einsum(
        "emt,td->emd", picker.astype(jnp.bfloat16), normed, preferred_element_type=jnp.float32
    ).astype(jnp.bfloat16)
    arrived_rows = [pick_block(outgoing, own_group)]
    arrived_shares = [pick_block(shares, own_group)]
    for stride in range(1, EXPERTS):
        target = (own_group + stride) % EXPERTS
        rows_in, shares_in = (
            from_behind(pick_block(outgoing, target), "expert", stride * group_width),
            from_behind(
                pick_block(shares, target).astype(jnp.bfloat16), "expert", stride * group_width
            ).astype(jnp.float32),
        )
        arrived_rows.append(rows_in)
        arrived_shares.append(shares_in)
    home_order = (own_group - jnp.arange(EXPERTS, dtype=jnp.int32)) % EXPERTS
    rows_by_source = jnp.take(jnp.stack(arrived_rows), home_order, axis=0)
    shares_by_source = jnp.take(jnp.stack(arrived_shares), home_order, axis=0)
    kept_rows, kept_shares = spread(
        rows_by_source[None], shares_by_source[None], own_index, level_values
    )
    slot_rows = kept_rows.reshape(-1, kept_rows.shape[-1])
    slot_shares = kept_shares.reshape(-1)
    gate_part = jnp.dot(slot_rows, w_in[0], preferred_element_type=jnp.float32)
    up_part = jnp.dot(slot_rows, w_in[1], preferred_element_type=jnp.float32)
    hidden = (jax.nn.silu(gate_part) * up_part * slot_shares[:, None]).astype(jnp.bfloat16)
    return (stream_part, hidden)


def solution(mesh):
    placed = (
        P(("groups", "expert"), "sub"),
        P(("groups", "expert"), "sub"),
        P(None, ("groups", "expert"), "sub"),
        P(None, ("groups", "expert"), None, "sub"),
        P(("groups", "expert"), None),
        P(("groups", "expert")),
        P(),
        P(),
        P(("groups", "expert"), None),
        P(None, None, ("expert", "sub")),
    )
    return jax.shard_map(
        shards,
        mesh=mesh,
        in_specs=placed,
        out_specs=(P(("groups", "expert"), "sub"), P("groups", ("expert", "sub"))),
        check_vma=False,
    )
```

profile of v0, /device:TPU:25, one launch (start us, length us, event | category | flops | bytes accessed | tf_op | source)
XLA Modules:
  0.0 103.8 jit_solution(13297511967904677882)
XLA Ops:
  0.7 0.7 fusion.77
  1.5 0.7 copy.83
  2.2 5.5 %all-to-all-start = ((s32[8,1,1]{2,1,0:T(1,128)}), s32[8,1,1]{2,1,0:T(1,128)S(1)}, u32[]{:S(2)}, u32[]{:S(2)}) async-start(s32[8,1,1]{2,1,0:T(1,128)} %copy.83), calls=%async_computation | async-start | bytes 8192 | tf_op jit(solution)/shard_map/all_to_all | solution.py:97
  7.7 0.7 fusion.60
  8.4 0.7 bitcast_or_fusion
  9.0 0.8 copy.90
  11.4 0.7 compare_and_fusion.1
  12.1 1.3 %gather_fusion = bf16[8,2,4,512]{3,2,1,0:T(4,128)(2,1)S(1)} fusion(bf16[2,2,4,512]{3,2,1,0:T(4,128)(2,1)} %param.13, s32[1024]{0:T(1024)S(1)} %pad_clamp_fusion.2), kind=kCustom, calls=%fused_computation | custom fusion | bytes 131104 | tf_op jit(solution)/shard_map/jit(_take)/gather | solution.py:98
  13.4 0.7 select_bitcast_fusion
  14.1 5.4 %all-to-all-start.1 = ((bf16[2,8,4,512]{3,2,0,1:T(4,128)(2,1)}), bf16[2,8,4,512]{3,2,0,1:T(4,128)(2,1)S(1)}, u32[]{:S(2)}, u32[]{:S(2)}) async-start(bf16[2,8,4,512]{3,2,0,1:T(4,128)(2,1)} %select_bitcast_fusion), calls=%async_computation.1 | async-start | bytes 131072 | tf_op jit(solution)/shard_map/all_to_all | solution.py:99
  20.2 2.1 %all-to-all-done.1 = bf16[2,8,4,512]{3,2,0,1:T(4,128)(2,1)S(1)} async-done(((bf16[2,8,4,512]{3,2,0,1:T(4,128)(2,1)}), bf16[2,8,4,512]{3,2,0,1:T(4,128)(2,1)S(1)}, u32[]{:S(2)}, u32[]{:S(2)}) %all-to-all-start.1) | async-done | bytes 65568 | tf_op jit(solution)/shard_map/all_to_all | solution.py:99
  23.9 1.4 %fusion.21 = f32[64,4,3,128]{3,0,2,1:T(8,128)S(1)} fusion(f32[4,3,64]{2,1,0:T(4,128)S(1)} %fusion.81, bf16[96,4,128,1]{2,1,0,3:T(4,128)(2,1)S(1)} %bitcast.148, f32[4,3,64,96]{3,2,1,0:T(8,128)S(1)} %fusion.19), kind=kOutput, calls=%fused_computation.24 | convolution fusion | flops 19293024 | bytes 789504 | tf_op jit(solution)/shard_map/kgtl,lkd->tkgd/dot_general | solution.py:50
  26.4 4.6 %all_gather.3 = bf16[64,3072]{1,0:T(8,128)(2,1)S(1)} all-gather(bf16[64,1536]{1,0:T(8,128)(2,1)S(1)} %add_convert_fusion), channel_id=1, replica_groups=mesh['groups'=2,'expert'=8,'sub'=2] {'sub'}, dimensions={1}, use_global_device_ids=true | all-gather | bytes 589824 | tf_op jit(solution)/shard_map/all_gather | solution.py:107
  31.4 1.0 gather_fusion.4
  33.3 1.0 collective-permute-start.13
  34.3 1.5 %collective-permute-start.12 = (bf16[17]{0:T(256)(128)(2,1)S(1)}, bf16[17]{0:T(256)(128)(2,1)S(1)}, u32[]{:S(2)}, u32[]{:S(2)}) collective-permute-start(bf16[17]{0:T(256)(128)(2,1)S(1)} %get-tuple-element.13), channel_id=1, source_target_pairs={{0,12},{2,14},{4,0},{6,2},{8,4},{10,6},{12,8},{14,10},{1,13},{3,15... | collective-permute-start | bytes 110 | tf_op jit(solution)/shard_map/ppermute | solution.py:28
  35.8 2.0 %collective-permute-start.11 = (bf16[17]{0:T(256)(128)(2,1)S(1)}, bf16[17]{0:T(256)(128)(2,1)S(1)}, u32[]{:S(2)}, u32[]{:S(2)}) collective-permute-start(bf16[17]{0:T(256)(128)(2,1)S(1)} %get-tuple-element.14), channel_id=1, source_target_pairs={{0,10},{2,12},{4,14},{6,0},{8,2},{10,4},{12,6},{14,8},{1,11},{3,13... | collective-permute-start | bytes 110 | tf_op jit(solution)/shard_map/ppermute | solution.py:28
  38.0 2.4 %collective-permute-start.9 = (bf16[17]{0:T(256)(128)(2,1)S(1)}, bf16[17]{0:T(256)(128)(2,1)S(1)}, u32[]{:S(2)}, u32[]{:S(2)}) collective-permute-start(bf16[17]{0:T(256)(128)(2,1)S(1)} %get-tuple-element.16), channel_id=1, source_target_pairs={{0,6},{2,8},{4,10},{6,12},{8,14},{10,0},{12,2},{14,4},{1,7},{3,9},... | collective-permute-start | bytes 110 | tf_op jit(solution)/shard_map/ppermute | solution.py:28
  40.4 0.6 convolution_convert_fusion
  41.1 0.8 collective-permute-start.8
  42.0 1.0 collective-permute-start.7
  43.0 1.4 %collective-permute-start.6 = (bf16[17,3072]{1,0:T(8,128)(2,1)S(1)}, bf16[17,3072]{1,0:T(8,128)(2,1)S(1)}, u32[]{:S(2)}, u32[]{:S(2)}) collective-permute-start(bf16[17,3072]{1,0:T(8,128)(2,1)S(1)} %get-tuple-element.2), channel_id=1, source_target_pairs={{0,14},{2,0},{4,2},{6,4},{8,6},{10,8},{12,10},{14,12},{1,15},{3,1}... | collective-permute-start | bytes 313352 | tf_op jit(solution)/shard_map/ppermute | solution.py:28
  44.3 0.7 collective-permute-start.5
  45.1 2.9 %collective-permute-start.3 = (bf16[17,3072]{1,0:T(8,128)(2,1)S(1)}, bf16[17,3072]{1,0:T(8,128)(2,1)S(1)}, u32[]{:S(2)}, u32[]{:S(2)}) collective-permute-start(bf16[17,3072]{1,0:T(8,128)(2,1)S(1)} %get-tuple-element.5), channel_id=1, source_target_pairs={{0,8},{2,10},{4,12},{6,14},{8,0},{10,2},{12,4},{14,6},{1,9},{3,11}... | collective-permute-start | bytes 313352 | tf_op jit(solution)/shard_map/ppermute | solution.py:28
  48.0 1.2 %collective-permute-start = (bf16[17,3072]{1,0:T(8,128)(2,1)S(1)}, bf16[17,3072]{1,0:T(8,128)(2,1)S(1)}, u32[]{:S(2)}, u32[]{:S(2)}) collective-permute-start(bf16[17,3072]{1,0:T(8,128)(2,1)S(1)} %get-tuple-element.8), channel_id=1, source_target_pairs={{0,2},{2,4},{4,6},{6,8},{8,10},{10,12},{12,14},{14,0},{1,3},{3,5},... | collective-permute-start | bytes 313352 | tf_op jit(solution)/shard_map/ppermute | solution.py:28
  49.9 8.6 %collective-permute-done = bf16[17,3072]{1,0:T(8,128)(2,1)S(1)} collective-permute-done((bf16[17,3072]{1,0:T(8,128)(2,1)S(1)}, bf16[17,3072]{1,0:T(8,128)(2,1)S(1)}, u32[]{:S(2)}, u32[]{:S(2)}) %collective-permute-start) | collective-permute-done | bytes 104480 | tf_op jit(solution)/shard_map/ppermute | solution.py:28
  58.5 1.0 collective-permute-start.1
  59.5 11.4 %collective-permute-done.1 = bf16[17,3072]{1,0:T(8,128)(2,1)S(1)} collective-permute-done((bf16[17,3072]{1,0:T(8,128)(2,1)S(1)}, bf16[17,3072]{1,0:T(8,128)(2,1)S(1)}, u32[]{:S(2)}, u32[]{:S(2)}) %collective-permute-start.1) | collective-permute-done | bytes 104480 | tf_op jit(solution)/shard_map/ppermute | solution.py:28
  70.9 10.3 %collective-permute-done.2 = bf16[17,3072]{1,0:T(8,128)(2,1)S(1)} collective-permute-done((bf16[17,3072]{1,0:T(8,128)(2,1)S(1)}, bf16[17,3072]{1,0:T(8,128)(2,1)S(1)}, u32[]{:S(2)}, u32[]{:S(2)}) %collective-permute-start.2) | collective-permute-done | bytes 104480 | tf_op jit(solution)/shard_map/ppermute | solution.py:28
  81.3 0.6 gather_fusion.2
  82.4 10.1 %fusion.3 = f32[136,4096]{1,0:T(8,128)S(1)} fusion(bf16[136,3072]{1,0:T(8,128)(2,1)S(1)} %select_n.256, bf16[2,3072,4096]{2,1,0:T(8,128)(2,1)} %param.19), kind=kOutput, calls=%fused_computation.8 | convolution fusion | flops 3422552064 | bytes 28229632 | tf_op jit(solution)/shard_map/dot_general | solution.py:153
  92.5 11.3 %fusion.13 = bf16[136,4096]{1,0:T(8,128)(2,1)} fusion(bf16[136,3072]{1,0:T(8,128)(2,1)S(1)} %select_n.256, bf16[2,3072,4096]{2,1,0:T(8,128)(2,1)} %param.19, f32[136,4096]{1,0:T(8,128)S(1)} %fusion.3, f32[136]{0:T(256)S(1)} %select_n.260), kind=kOutput, calls=%fused_computation.14 | convolution fusion | flops 3426451456 | bytes 29344288 | tf_op jit(solution)/shard_map/dot_general | solution.py:154
  (99 shorter events, 7.0 us)
Async XLA Ops:
  0.6 30.5 %copy-start = (bf16[3072,8]{0,1:T(8,128)(2,1)S(1)}, bf16[3072,8]{0,1:T(8,128)(2,1)}, u32[]{:S(2)}) copy-start(bf16[3072,8]{0,1:T(8,128)(2,1)} %param.17) | copy-start | bytes 147460
  0.6 19.2 %copy-start.2 = (bf16[64,1536]{1,0:T(8,128)(2,1)S(1)}, bf16[64,1536]{1,0:T(8,128)(2,1)}, u32[]{:S(2)}) copy-start(bf16[64,1536]{1,0:T(8,128)(2,1)} %param.11) | copy-start | bytes 589828
  0.7 22.5 %copy-start.4 = (bf16[2,64,512]{2,1,0:T(8,128)(2,1)S(1)}, bf16[2,64,512]{2,1,0:T(8,128)(2,1)}, u32[]{:S(2)}) copy-start(bf16[2,64,512]{2,1,0:T(8,128)(2,1)} %param.12) | copy-start | bytes 393220
  2.2 8.9 %all-to-all-start = ((s32[8,1,1]{2,1,0:T(1,128)}), s32[8,1,1]{2,1,0:T(1,128)S(1)}, u32[]{:S(2)}, u32[]{:S(2)}) async-start(s32[8,1,1]{2,1,0:T(1,128)} %copy.83), calls=%async_computation | async-start | bytes 8192 | tf_op jit(solution)/shard_map/all_to_all | solution.py:97
  14.1 8.2 %all-to-all-start.1 = ((bf16[2,8,4,512]{3,2,0,1:T(4,128)(2,1)}), bf16[2,8,4,512]{3,2,0,1:T(4,128)(2,1)S(1)}, u32[]{:S(2)}, u32[]{:S(2)}) async-start(bf16[2,8,4,512]{3,2,0,1:T(4,128)(2,1)} %select_bitcast_fusion), calls=%async_computation.1 | async-start | bytes 131072 | tf_op jit(solution)/shard_map/all_to_all | solution.py:99
  25.4 0.9 copy-start.3
  25.6 5.5 %copy-start.5 = (f32[3072]{0:T(1024)S(1)}, f32[3072]{0:T(1024)}, u32[]{:S(2)}) copy-start(f32[3072]{0:T(1024)} %param.16) | copy-start | bytes 36868
  26.3 6.1 %copy-start.1 = (bf16[64,1536]{1,0:T(8,128)(2,1)}, bf16[64,1536]{1,0:T(8,128)(2,1)S(1)}, u32[]{:S(2)}) copy-start(bf16[64,1536]{1,0:T(8,128)(2,1)S(1)} %add_convert_fusion) | copy-start | bytes 589828
  31.4 1.3 %copy-start.6 = (s32[64,2]{0,1:T(2,128)S(1)}, s32[64,2]{0,1:T(2,128)}, u32[]{:S(2)}) copy-start(s32[64,2]{0,1:T(2,128)} %param.18) | copy-start | bytes 1540
  33.3 7.8 %collective-permute-start.13 = (bf16[17]{0:T(256)(128)(2,1)S(1)}, bf16[17]{0:T(256)(128)(2,1)S(1)}, u32[]{:S(2)}, u32[]{:S(2)}) collective-permute-start(bf16[17]{0:T(256)(128)(2,1)S(1)} %get-tuple-element.12), channel_id=1, source_target_pairs={{0,14},{2,0},{4,2},{6,4},{8,6},{10,8},{12,10},{14,12},{1,15},{3,1}... | collective-permute-start | bytes 110 | tf_op jit(solution)/shard_map/ppermute | solution.py:28
  34.3 7.7 %collective-permute-start.12 = (bf16[17]{0:T(256)(128)(2,1)S(1)}, bf16[17]{0:T(256)(128)(2,1)S(1)}, u32[]{:S(2)}, u32[]{:S(2)}) collective-permute-start(bf16[17]{0:T(256)(128)(2,1)S(1)} %get-tuple-element.13), channel_id=1, source_target_pairs={{0,12},{2,14},{4,0},{6,2},{8,4},{10,6},{12,8},{14,10},{1,13},{3,15... | collective-permute-start | bytes 110 | tf_op jit(solution)/shard_map/ppermute | solution.py:28
  35.8 7.2 %collective-permute-start.11 = (bf16[17]{0:T(256)(128)(2,1)S(1)}, bf16[17]{0:T(256)(128)(2,1)S(1)}, u32[]{:S(2)}, u32[]{:S(2)}) collective-permute-start(bf16[17]{0:T(256)(128)(2,1)S(1)} %get-tuple-element.14), channel_id=1, source_target_pairs={{0,10},{2,12},{4,14},{6,0},{8,2},{10,4},{12,6},{14,8},{1,11},{3,13... | collective-permute-start | bytes 110 | tf_op jit(solution)/shard_map/ppermute | solution.py:28
  37.8 6.6 %collective-permute-start.10 = (bf16[17]{0:T(256)(128)(2,1)S(1)}, bf16[17]{0:T(256)(128)(2,1)S(1)}, u32[]{:S(2)}, u32[]{:S(2)}) collective-permute-start(bf16[17]{0:T(256)(128)(2,1)S(1)} %get-tuple-element.15), channel_id=1, source_target_pairs={{0,8},{2,10},{4,12},{6,14},{8,0},{10,2},{12,4},{14,6},{1,9},{3,11}... | collective-permute-start | bytes 110 | tf_op jit(solution)/shard_map/ppermute | solution.py:28
  38.0 7.0 %collective-permute-start.9 = (bf16[17]{0:T(256)(128)(2,1)S(1)}, bf16[17]{0:T(256)(128)(2,1)S(1)}, u32[]{:S(2)}, u32[]{:S(2)}) collective-permute-start(bf16[17]{0:T(256)(128)(2,1)S(1)} %get-tuple-element.16), channel_id=1, source_target_pairs={{0,6},{2,8},{4,10},{6,12},{8,14},{10,0},{12,2},{14,4},{1,7},{3,9},... | collective-permute-start | bytes 110 | tf_op jit(solution)/shard_map/ppermute | solution.py:28
  41.1 3.9 %collective-permute-start.8 = (bf16[17]{0:T(256)(128)(2,1)S(1)}, bf16[17]{0:T(256)(128)(2,1)S(1)}, u32[]{:S(2)}, u32[]{:S(2)}) collective-permute-start(bf16[17]{0:T(256)(128)(2,1)S(1)} %get-tuple-element.17), channel_id=1, source_target_pairs={{0,4},{2,6},{4,8},{6,10},{8,12},{10,14},{12,0},{14,2},{1,5},{3,7},... | collective-permute-start | bytes 110 | tf_op jit(solution)/shard_map/ppermute | solution.py:28
  42.0 6.0 %collective-permute-start.7 = (bf16[17]{0:T(256)(128)(2,1)S(1)}, bf16[17]{0:T(256)(128)(2,1)S(1)}, u32[]{:S(2)}, u32[]{:S(2)}) collective-permute-start(bf16[17]{0:T(256)(128)(2,1)S(1)} %get-tuple-element.18), channel_id=1, source_target_pairs={{0,2},{2,4},{4,6},{6,8},{8,10},{10,12},{12,14},{14,0},{1,3},{3,5},... | collective-permute-start | bytes 110 | tf_op jit(solution)/shard_map/ppermute | solution.py:28
  43.0 38.3 %collective-permute-start.6 = (bf16[17,3072]{1,0:T(8,128)(2,1)S(1)}, bf16[17,3072]{1,0:T(8,128)(2,1)S(1)}, u32[]{:S(2)}, u32[]{:S(2)}) collective-permute-start(bf16[17,3072]{1,0:T(8,128)(2,1)S(1)} %get-tuple-element.2), channel_id=1, source_target_pairs={{0,14},{2,0},{4,2},{6,4},{8,6},{10,8},{12,10},{14,12},{1,15},{3,1}... | collective-permute-start | bytes 313352 | tf_op jit(solution)/shard_map/ppermute | solution.py:28
  44.3 36.9 %collective-permute-start.5 = (bf16[17,3072]{1,0:T(8,128)(2,1)S(1)}, bf16[17,3072]{1,0:T(8,128)(2,1)S(1)}, u32[]{:S(2)}, u32[]{:S(2)}) collective-permute-start(bf16[17,3072]{1,0:T(8,128)(2,1)S(1)} %get-tuple-element.3), channel_id=1, source_target_pairs={{0,12},{2,14},{4,0},{6,2},{8,4},{10,6},{12,8},{14,10},{1,13},{3,15... | collective-permute-start | bytes 313352 | tf_op jit(solution)/shard_map/ppermute | solution.py:28
  45.0 36.2 %collective-permute-start.4 = (bf16[17,3072]{1,0:T(8,128)(2,1)S(1)}, bf16[17,3072]{1,0:T(8,128)(2,1)S(1)}, u32[]{:S(2)}, u32[]{:S(2)}) collective-permute-start(bf16[17,3072]{1,0:T(8,128)(2,1)S(1)} %get-tuple-element.4), channel_id=1, source_target_pairs={{0,10},{2,12},{4,14},{6,0},{8,2},{10,4},{12,6},{14,8},{1,11},{3,13... | collective-permute-start | bytes 313352 | tf_op jit(solution)/shard_map/ppermute | solution.py:28
  45.1 36.1 %collective-permute-start.3 = (bf16[17,3072]{1,0:T(8,128)(2,1)S(1)}, bf16[17,3072]{1,0:T(8,128)(2,1)S(1)}, u32[]{:S(2)}, u32[]{:S(2)}) collective-permute-start(bf16[17,3072]{1,0:T(8,128)(2,1)S(1)} %get-tuple-element.5), channel_id=1, source_target_pairs={{0,8},{2,10},{4,12},{6,14},{8,0},{10,2},{12,4},{14,6},{1,9},{3,11}... | collective-permute-start | bytes 313352 | tf_op jit(solution)/shard_map/ppermute | solution.py:28
  48.0 10.5 %collective-permute-start = (bf16[17,3072]{1,0:T(8,128)(2,1)S(1)}, bf16[17,3072]{1,0:T(8,128)(2,1)S(1)}, u32[]{:S(2)}, u32[]{:S(2)}) collective-permute-start(bf16[17,3072]{1,0:T(8,128)(2,1)S(1)} %get-tuple-element.8), channel_id=1, source_target_pairs={{0,2},{2,4},{4,6},{6,8},{8,10},{10,12},{12,14},{14,0},{1,3},{3,5},... | collective-permute-start | bytes 313352 | tf_op jit(solution)/shard_map/ppermute | solution.py:28
  58.5 12.4 %collective-permute-start.1 = (bf16[17,3072]{1,0:T(8,128)(2,1)S(1)}, bf16[17,3072]{1,0:T(8,128)(2,1)S(1)}, u32[]{:S(2)}, u32[]{:S(2)}) collective-permute-start(bf16[17,3072]{1,0:T(8,128)(2,1)S(1)} %get-tuple-element.7), channel_id=1, source_target_pairs={{0,4},{2,6},{4,8},{6,10},{8,12},{10,14},{12,0},{14,2},{1,5},{3,7},... | collective-permute-start | bytes 313352 | tf_op jit(solution)/shard_map/ppermute | solution.py:28
  70.9 10.3 %collective-permute-start.2 = (bf16[17,3072]{1,0:T(8,128)(2,1)S(1)}, bf16[17,3072]{1,0:T(8,128)(2,1)S(1)}, u32[]{:S(2)}, u32[]{:S(2)}) collective-permute-start(bf16[17,3072]{1,0:T(8,128)(2,1)S(1)} %get-tuple-element.6), channel_id=1, source_target_pairs={{0,6},{2,8},{4,10},{6,12},{8,14},{10,0},{12,2},{14,4},{1,7},{3,9},... | collective-permute-start | bytes 313352 | tf_op jit(solution)/shard_map/ppermute | solution.py:28
where the time goes:
time: 104 us
  waiting for transfers between devices  32.4 us (31%)
  starting transfers between devices  26.9 us (26%)
  matrix products  24.5 us (24%)
  local copies, waits for them, and re-layouts  8.52 us (8%)
  other arithmetic  5 us (5%)
  blocking collectives  4.6 us (4%)
  between operations  1.78 us (2%)
    ppermute x14, waiting for transfers between devices, from_behind(): return lax.ppermute(value, axis, pairs)  30.3 us
    ppermute x14, starting transfers between devices, from_behind(): return lax.ppermute(value, axis, pairs)  16 us
    dot_general x1, matrix products, shards(): up_part = jnp.dot(slot_rows, w_in[1], preferred_element_type=jnp.float32)  11.3 us
    dot_general x1, matrix products, shards(): gate_part = jnp.dot(slot_rows, w_in[0], preferred_element_type=jnp.float32)  10.1 us
    all_to_all x1, starting transfers between devices, shards(): lax.all_to_all(wanted[:, None], 'expert', split_axis=0, concat_axis=0, ti...  5.47 us
    all_to_all x1, starting transfers between devices, shards(): lax.all_to_all(served, 'expert', split_axis=1, concat_axis=1, tiled=True)  5.44 us
    all_gather x1, blocking collectives, shards(): stream = lax.all_gather(stream_part, 'sub', axis=1, tiled=True)  4.6 us
    all_to_all x1, waiting for transfers between devices, shards(): lax.all_to_all(served, 'expert', split_axis=1, concat_axis=1, tiled=True)  2.11 us
  transfers between devices with their start and end apart: 16, of which 4 were waited for; matrix products, arithmetic and copies ran while one was open for 5% of the time, Pallas kernels for 0%

commit v1 on v0

--- a/solution.py
+++ b/solution.py
@@ -96,7 +96,12 @@
     wanted = jnp.sum(jnp.where(owner_hot, inside[None, :], 0), axis=1)
     asked_for = lax.all_to_all(wanted[:, None], "expert", split_axis=0, concat_axis=0, tiled=True)
     served = jnp.take(paged_key_value_cache, asked_for[:, 0], axis=1)
-    arrived = lax.all_to_all(served, "expert", split_axis=1, concat_axis=1, tiled=True)
+    arrived = jnp.concatenate(
+        lax.all_to_all(
+            jnp.stack(jnp.split(served, lax.axis_size("expert"), axis=1)), "expert", 0, 0
+        ),
+        axis=1,
+    )
     prefix_pages = jnp.take(arrived, owners, axis=1)
     prefix_row_block = prefix_pages.reshape(2, -1, prefix_pages.shape[-1])
     key_rows = jnp.concatenate([prefix_row_block, kv_new], axis=1)

time: 104 us -> 108 us (1.038)
  local copies, waits for them, and re-layouts: 8.52 us -> 13.3 us
    unnamed x22 -> x29, local copies, waits for them, and re-layouts: 1.3 us -> 5.52 us
where the time goes in v1:
time: 108 us
  waiting for transfers between devices  32.4 us (30%)
  starting transfers between devices  26.9 us (25%)
  matrix products  24.5 us (23%)
  local copies, waits for them, and re-layouts  13.3 us (12%)
  blocking collectives  4.6 us (4%)
  other arithmetic  4.36 us (4%)
  between operations  1.78 us (2%)
    ppermute x14, waiting for transfers between devices, from_behind(): return lax.ppermute(value, axis, pairs)  30.3 us
    ppermute x14, starting transfers between devices, from_behind(): return lax.ppermute(value, axis, pairs)  16 us
    dot_general x1, matrix products, shards(): up_part = jnp.dot(slot_rows, w_in[1], preferred_element_type=jnp.float32)  11.3 us
    dot_general x1, matrix products, shards(): gate_part = jnp.dot(slot_rows, w_in[0], preferred_element_type=jnp.float32)  10.1 us
    unnamed x29, local copies, waits for them, and re-layouts  5.52 us
    all_to_all x1, starting transfers between devices, shards(): lax.all_to_all(wanted[:, None], 'expert', split_axis=0, concat_axis=0, ti...  5.47 us
    all_to_all x1, starting transfers between devices, shards(): lax.all_to_all(jnp.stack(jnp.split(served, lax.axis_size('expert'), axis=...  5.44 us
    all_gather x1, blocking collectives, shards(): stream = lax.all_gather(stream_part, 'sub', axis=1, tiled=True)  4.6 us
  transfers between devices with their start and end apart: 16, of which 4 were waited for; matrix products, arithmetic and copies ran while one was open for 5% of the time, Pallas kernels for 0%

profile of v1, /device:TPU:25, one launch (start us, length us, event | category | flops | bytes accessed | tf_op | source)
XLA Modules:
  0.0 108.0 jit_solution(3128092927539208967)
XLA Ops:
  0.7 0.7 fusion.77
  1.5 0.7 copy.83
  2.2 5.5 %all-to-all-start = ((s32[8,1,1]{2,1,0:T(1,128)}), s32[8,1,1]{2,1,0:T(1,128)S(1)}, u32[]{:S(2)}, u32[]{:S(2)}) async-start(s32[8,1,1]{2,1,0:T(1,128)} %copy.83), calls=%async_computation | async-start | bytes 8192 | tf_op jit(solution)/shard_map/all_to_all | solution.py:97
  7.7 0.7 fusion.60
  8.3 0.7 bitcast_or_fusion
  9.0 0.8 copy.90
  11.3 0.7 compare_and_fusion.1
  12.0 1.3 %gather_fusion = bf16[8,2,4,512]{3,2,1,0:T(4,128)(2,1)S(1)} fusion(bf16[2,2,4,512]{3,2,1,0:T(4,128)(2,1)} %param.13, s32[1024]{0:T(1024)S(1)} %pad_clamp_fusion.2), kind=kCustom, calls=%fused_computation | custom fusion | bytes 131104 | tf_op jit(solution)/shard_map/jit(_take)/gather | solution.py:98
  18.3 5.4 %all-to-all-start.1 = ((bf16[8,2,1,4,512]{4,3,1,2,0:T(4,128)(2,1)}), bf16[8,2,1,4,512]{4,3,1,2,0:T(4,128)(2,1)S(1)}, u32[]{:S(2)}, u32[]{:S(2)}) async-start(bf16[8,2,1,4,512]{4,3,1,2,0:T(4,128)(2,1)} %constant_dynamic-update-slice_fusion), calls=%async_computation.1 | async-start | bytes 131072 | tf_op jit(solution)/shard_map/all_to_all | solution.py:100
  24.4 2.1 %all-to-all-done.1 = bf16[8,2,1,4,512]{4,3,1,2,0:T(4,128)(2,1)S(1)} async-done(((bf16[8,2,1,4,512]{4,3,1,2,0:T(4,128)(2,1)}), bf16[8,2,1,4,512]{4,3,1,2,0:T(4,128)(2,1)S(1)}, u32[]{:S(2)}, u32[]{:S(2)}) %all-to-all-start.1) | async-done | bytes 65568 | tf_op jit(solution)/shard_map/all_to_all | solution.py:100
  26.5 0.6 gather_fusion.1
  28.1 1.4 %fusion.21 = f32[64,4,3,128]{3,0,2,1:T(8,128)S(1)} fusion(f32[4,3,64]{2,1,0:T(4,128)S(1)} %fusion.81, bf16[96,4,128,1]{2,1,0,3:T(4,128)(2,1)S(1)} %bitcast.184, f32[4,3,64,96]{3,2,1,0:T(8,128)S(1)} %fusion.19), kind=kOutput, calls=%fused_computation.24 | convolution fusion | flops 19293024 | bytes 789504 | tf_op jit(solution)/shard_map/kgtl,lkd->tkgd/dot_general | solution.py:50
  30.5 4.6 %all_gather.3 = bf16[64,3072]{1,0:T(8,128)(2,1)S(1)} all-gather(bf16[64,1536]{1,0:T(8,128)(2,1)S(1)} %add_convert_fusion), channel_id=1, replica_groups=mesh['groups'=2,'expert'=8,'sub'=2] {'sub'}, dimensions={1}, use_global_device_ids=true | all-gather | bytes 589824 | tf_op jit(solution)/shard_map/all_gather | solution.py:112
  35.6 1.0 gather_fusion.4
  37.5 1.0 collective-permute-start.13
  38.4 1.5 %collective-permute-start.12 = (bf16[17]{0:T(256)(128)(2,1)S(1)}, bf16[17]{0:T(256)(128)(2,1)S(1)}, u32[]{:S(2)}, u32[]{:S(2)}) collective-permute-start(bf16[17]{0:T(256)(128)(2,1)S(1)} %get-tuple-element.13), channel_id=1, source_target_pairs={{0,12},{2,14},{4,0},{6,2},{8,4},{10,6},{12,8},{14,10},{1,13},{3,15... | collective-permute-start | bytes 110 | tf_op jit(solution)/shard_map/ppermute | solution.py:28
  40.0 2.0 %collective-permute-start.11 = (bf16[17]{0:T(256)(128)(2,1)S(1)}, bf16[17]{0:T(256)(128)(2,1)S(1)}, u32[]{:S(2)}, u32[]{:S(2)}) collective-permute-start(bf16[17]{0:T(256)(128)(2,1)S(1)} %get-tuple-element.14), channel_id=1, source_target_pairs={{0,10},{2,12},{4,14},{6,0},{8,2},{10,4},{12,6},{14,8},{1,11},{3,13... | collective-permute-start | bytes 110 | tf_op jit(solution)/shard_map/ppermute | solution.py:28
  42.2 2.4 %collective-permute-start.9 = (bf16[17]{0:T(256)(128)(2,1)S(1)}, bf16[17]{0:T(256)(128)(2,1)S(1)}, u32[]{:S(2)}, u32[]{:S(2)}) collective-permute-start(bf16[17]{0:T(256)(128)(2,1)S(1)} %get-tuple-element.16), channel_id=1, source_target_pairs={{0,6},{2,8},{4,10},{6,12},{8,14},{10,0},{12,2},{14,4},{1,7},{3,9},... | collective-permute-start | bytes 110 | tf_op jit(solution)/shard_map/ppermute | solution.py:28
  44.6 0.6 convolution_convert_fusion
  45.3 0.8 collective-permute-start.8
  46.1 1.0 collective-permute-start.7
  47.2 1.4 %collective-permute-start.6 = (bf16[17,3072]{1,0:T(8,128)(2,1)S(1)}, bf16[17,3072]{1,0:T(8,128)(2,1)S(1)}, u32[]{:S(2)}, u32[]{:S(2)}) collective-permute-start(bf16[17,3072]{1,0:T(8,128)(2,1)S(1)} %get-tuple-element.2), channel_id=1, source_target_pairs={{0,14},{2,0},{4,2},{6,4},{8,6},{10,8},{12,10},{14,12},{1,15},{3,1}... | collective-permute-start | bytes 313352 | tf_op jit(solution)/shard_map/ppermute | solution.py:28
  48.5 0.7 collective-permute-start.5
  49.2 2.9 %collective-permute-start.3 = (bf16[17,3072]{1,0:T(8,128)(2,1)S(1)}, bf16[17,3072]{1,0:T(8,128)(2,1)S(1)}, u32[]{:S(2)}, u32[]{:S(2)}) collective-permute-start(bf16[17,3072]{1,0:T(8,128)(2,1)S(1)} %get-tuple-element.5), channel_id=1, source_target_pairs={{0,8},{2,10},{4,12},{6,14},{8,0},{10,2},{12,4},{14,6},{1,9},{3,11}... | collective-permute-start | bytes 313352 | tf_op jit(solution)/shard_map/ppermute | solution.py:28
  52.2 1.2 %collective-permute-start = (bf16[17,3072]{1,0:T(8,128)(2,1)S(1)}, bf16[17,3072]{1,0:T(8,128)(2,1)S(1)}, u32[]{:S(2)}, u32[]{:S(2)}) collective-permute-start(bf16[17,3072]{1,0:T(8,128)(2,1)S(1)} %get-tuple-element.8), channel_id=1, source_target_pairs={{0,2},{2,4},{4,6},{6,8},{8,10},{10,12},{12,14},{14,0},{1,3},{3,5},... | collective-permute-start | bytes 313352 | tf_op jit(solution)/shard_map/ppermute | solution.py:28
  54.1 8.6 %collective-permute-done = bf16[17,3072]{1,0:T(8,128)(2,1)S(1)} collective-permute-done((bf16[17,3072]{1,0:T(8,128)(2,1)S(1)}, bf16[17,3072]{1,0:T(8,128)(2,1)S(1)}, u32[]{:S(2)}, u32[]{:S(2)}) %collective-permute-start) | collective-permute-done | bytes 104480 | tf_op jit(solution)/shard_map/ppermute | solution.py:28
  62.7 1.0 collective-permute-start.1
  63.7 11.4 %collective-permute-done.1 = bf16[17,3072]{1,0:T(8,128)(2,1)S(1)} collective-permute-done((bf16[17,3072]{1,0:T(8,128)(2,1)S(1)}, bf16[17,3072]{1,0:T(8,128)(2,1)S(1)}, u32[]{:S(2)}, u32[]{:S(2)}) %collective-permute-start.1) | collective-permute-done | bytes 104480 | tf_op jit(solution)/shard_map/ppermute | solution.py:28
  75.1 10.3 %collective-permute-done.2 = bf16[17,3072]{1,0:T(8,128)(2,1)S(1)} collective-permute-done((bf16[17,3072]{1,0:T(8,128)(2,1)S(1)}, bf16[17,3072]{1,0:T(8,128)(2,1)S(1)}, u32[]{:S(2)}, u32[]{:S(2)}) %collective-permute-start.2) | collective-permute-done | bytes 104480 | tf_op jit(solution)/shard_map/ppermute | solution.py:28
  85.5 0.6 gather_fusion.2
  86.6 10.1 %fusion.3 = f32[136,4096]{1,0:T(8,128)S(1)} fusion(bf16[136,3072]{1,0:T(8,128)(2,1)S(1)} %select_n.256, bf16[2,3072,4096]{2,1,0:T(8,128)(2,1)} %param.19), kind=kOutput, calls=%fused_computation.8 | convolution fusion | flops 3422552064 | bytes 28229632 | tf_op jit(solution)/shard_map/dot_general | solution.py:158
  96.7 11.3 %fusion.13 = bf16[136,4096]{1,0:T(8,128)(2,1)} fusion(bf16[136,3072]{1,0:T(8,128)(2,1)S(1)} %select_n.256, bf16[2,3072,4096]{2,1,0:T(8,128)(2,1)} %param.19, f32[136,4096]{1,0:T(8,128)S(1)} %fusion.3, f32[136]{0:T(256)S(1)} %select_n.260), kind=kOutput, calls=%fused_computation.14 | convolution fusion | flops 3426451456 | bytes 29344288 | tf_op jit(solution)/shard_map/dot_general | solution.py:159
  (107 shorter events, 11.3 us)
Async XLA Ops:
  0.6 34.7 %copy-start = (bf16[3072,8]{0,1:T(8,128)(2,1)S(1)}, bf16[3072,8]{0,1:T(8,128)(2,1)}, u32[]{:S(2)}) copy-start(bf16[3072,8]{0,1:T(8,128)(2,1)} %param.17) | copy-start | bytes 147460
  0.6 23.4 %copy-start.2 = (bf16[64,1536]{1,0:T(8,128)(2,1)S(1)}, bf16[64,1536]{1,0:T(8,128)(2,1)}, u32[]{:S(2)}) copy-start(bf16[64,1536]{1,0:T(8,128)(2,1)} %param.11) | copy-start | bytes 589828
  1.5 25.9 %copy-start.4 = (bf16[2,64,512]{2,1,0:T(8,128)(2,1)S(1)}, bf16[2,64,512]{2,1,0:T(8,128)(2,1)}, u32[]{:S(2)}) copy-start(bf16[2,64,512]{2,1,0:T(8,128)(2,1)} %param.12) | copy-start | bytes 393220
  2.2 8.9 %all-to-all-start = ((s32[8,1,1]{2,1,0:T(1,128)}), s32[8,1,1]{2,1,0:T(1,128)S(1)}, u32[]{:S(2)}, u32[]{:S(2)}) async-start(s32[8,1,1]{2,1,0:T(1,128)} %copy.83), calls=%async_computation | async-start | bytes 8192 | tf_op jit(solution)/shard_map/all_to_all | solution.py:97
  18.3 8.2 %all-to-all-start.1 = ((bf16[8,2,1,4,512]{4,3,1,2,0:T(4,128)(2,1)}), bf16[8,2,1,4,512]{4,3,1,2,0:T(4,128)(2,1)S(1)}, u32[]{:S(2)}, u32[]{:S(2)}) async-start(bf16[8,2,1,4,512]{4,3,1,2,0:T(4,128)(2,1)} %constant_dynamic-update-slice_fusion), calls=%async_computation.1 | async-start | bytes 131072 | tf_op jit(solution)/shard_map/all_to_all | solution.py:100
  29.6 0.9 copy-start.3
  29.8 5.5 %copy-start.5 = (f32[3072]{0:T(1024)S(1)}, f32[3072]{0:T(1024)}, u32[]{:S(2)}) copy-start(f32[3072]{0:T(1024)} %param.16) | copy-start | bytes 36868
  30.5 6.1 %copy-start.1 = (bf16[64,1536]{1,0:T(8,128)(2,1)}, bf16[64,1536]{1,0:T(8,128)(2,1)S(1)}, u32[]{:S(2)}) copy-start(bf16[64,1536]{1,0:T(8,128)(2,1)S(1)} %add_convert_fusion) | copy-start | bytes 589828
  35.6 1.3 %copy-start.6 = (s32[64,2]{0,1:T(2,128)S(1)}, s32[64,2]{0,1:T(2,128)}, u32[]{:S(2)}) copy-start(s32[64,2]{0,1:T(2,128)} %param.18) | copy-start | bytes 1540
  37.5 7.8 %collective-permute-start.13 = (bf16[17]{0:T(256)(128)(2,1)S(1)}, bf16[17]{0:T(256)(128)(2,1)S(1)}, u32[]{:S(2)}, u32[]{:S(2)}) collective-permute-start(bf16[17]{0:T(256)(128)(2,1)S(1)} %get-tuple-element.12), channel_id=1, source_target_pairs={{0,14},{2,0},{4,2},{6,4},{8,6},{10,8},{12,10},{14,12},{1,15},{3,1}... | collective-permute-start | bytes 110 | tf_op jit(solution)/shard_map/ppermute | solution.py:28
  38.4 7.7 %collective-permute-start.12 = (bf16[17]{0:T(256)(128)(2,1)S(1)}, bf16[17]{0:T(256)(128)(2,1)S(1)}, u32[]{:S(2)}, u32[]{:S(2)}) collective-permute-start(bf16[17]{0:T(256)(128)(2,1)S(1)} %get-tuple-element.13), channel_id=1, source_target_pairs={{0,12},{2,14},{4,0},{6,2},{8,4},{10,6},{12,8},{14,10},{1,13},{3,15... | collective-permute-start | bytes 110 | tf_op jit(solution)/shard_map/ppermute | solution.py:28
  40.0 7.2 %collective-permute-start.11 = (bf16[17]{0:T(256)(128)(2,1)S(1)}, bf16[17]{0:T(256)(128)(2,1)S(1)}, u32[]{:S(2)}, u32[]{:S(2)}) collective-permute-start(bf16[17]{0:T(256)(128)(2,1)S(1)} %get-tuple-element.14), channel_id=1, source_target_pairs={{0,10},{2,12},{4,14},{6,0},{8,2},{10,4},{12,6},{14,8},{1,11},{3,13... | collective-permute-start | bytes 110 | tf_op jit(solution)/shard_map/ppermute | solution.py:28
  42.0 6.6 %collective-permute-start.10 = (bf16[17]{0:T(256)(128)(2,1)S(1)}, bf16[17]{0:T(256)(128)(2,1)S(1)}, u32[]{:S(2)}, u32[]{:S(2)}) collective-permute-start(bf16[17]{0:T(256)(128)(2,1)S(1)} %get-tuple-element.15), channel_id=1, source_target_pairs={{0,8},{2,10},{4,12},{6,14},{8,0},{10,2},{12,4},{14,6},{1,9},{3,11}... | collective-permute-start | bytes 110 | tf_op jit(solution)/shard_map/ppermute | solution.py:28
  42.2 7.0 %collective-permute-start.9 = (bf16[17]{0:T(256)(128)(2,1)S(1)}, bf16[17]{0:T(256)(128)(2,1)S(1)}, u32[]{:S(2)}, u32[]{:S(2)}) collective-permute-start(bf16[17]{0:T(256)(128)(2,1)S(1)} %get-tuple-element.16), channel_id=1, source_target_pairs={{0,6},{2,8},{4,10},{6,12},{8,14},{10,0},{12,2},{14,4},{1,7},{3,9},... | collective-permute-start | bytes 110 | tf_op jit(solution)/shard_map/ppermute | solution.py:28
  45.3 3.9 %collective-permute-start.8 = (bf16[17]{0:T(256)(128)(2,1)S(1)}, bf16[17]{0:T(256)(128)(2,1)S(1)}, u32[]{:S(2)}, u32[]{:S(2)}) collective-permute-start(bf16[17]{0:T(256)(128)(2,1)S(1)} %get-tuple-element.17), channel_id=1, source_target_pairs={{0,4},{2,6},{4,8},{6,10},{8,12},{10,14},{12,0},{14,2},{1,5},{3,7},... | collective-permute-start | bytes 110 | tf_op jit(solution)/shard_map/ppermute | solution.py:28
  46.1 6.0 %collective-permute-start.7 = (bf16[17]{0:T(256)(128)(2,1)S(1)}, bf16[17]{0:T(256)(128)(2,1)S(1)}, u32[]{:S(2)}, u32[]{:S(2)}) collective-permute-start(bf16[17]{0:T(256)(128)(2,1)S(1)} %get-tuple-element.18), channel_id=1, source_target_pairs={{0,2},{2,4},{4,6},{6,8},{8,10},{10,12},{12,14},{14,0},{1,3},{3,5},... | collective-permute-start | bytes 110 | tf_op jit(solution)/shard_map/ppermute | solution.py:28
  47.2 38.3 %collective-permute-start.6 = (bf16[17,3072]{1,0:T(8,128)(2,1)S(1)}, bf16[17,3072]{1,0:T(8,128)(2,1)S(1)}, u32[]{:S(2)}, u32[]{:S(2)}) collective-permute-start(bf16[17,3072]{1,0:T(8,128)(2,1)S(1)} %get-tuple-element.2), channel_id=1, source_target_pairs={{0,14},{2,0},{4,2},{6,4},{8,6},{10,8},{12,10},{14,12},{1,15},{3,1}... | collective-permute-start | bytes 313352 | tf_op jit(solution)/shard_map/ppermute | solution.py:28
  48.5 36.9 %collective-permute-start.5 = (bf16[17,3072]{1,0:T(8,128)(2,1)S(1)}, bf16[17,3072]{1,0:T(8,128)(2,1)S(1)}, u32[]{:S(2)}, u32[]{:S(2)}) collective-permute-start(bf16[17,3072]{1,0:T(8,128)(2,1)S(1)} %get-tuple-element.3), channel_id=1, source_target_pairs={{0,12},{2,14},{4,0},{6,2},{8,4},{10,6},{12,8},{14,10},{1,13},{3,15... | collective-permute-start | bytes 313352 | tf_op jit(solution)/shard_map/ppermute | solution.py:28
  49.2 36.2 %collective-permute-start.4 = (bf16[17,3072]{1,0:T(8,128)(2,1)S(1)}, bf16[17,3072]{1,0:T(8,128)(2,1)S(1)}, u32[]{:S(2)}, u32[]{:S(2)}) collective-permute-start(bf16[17,3072]{1,0:T(8,128)(2,1)S(1)} %get-tuple-element.4), channel_id=1, source_target_pairs={{0,10},{2,12},{4,14},{6,0},{8,2},{10,4},{12,6},{14,8},{1,11},{3,13... | collective-permute-start | bytes 313352 | tf_op jit(solution)/shard_map/ppermute | solution.py:28
  49.2 36.1 %collective-permute-start.3 = (bf16[17,3072]{1,0:T(8,128)(2,1)S(1)}, bf16[17,3072]{1,0:T(8,128)(2,1)S(1)}, u32[]{:S(2)}, u32[]{:S(2)}) collective-permute-start(bf16[17,3072]{1,0:T(8,128)(2,1)S(1)} %get-tuple-element.5), channel_id=1, source_target_pairs={{0,8},{2,10},{4,12},{6,14},{8,0},{10,2},{12,4},{14,6},{1,9},{3,11}... | collective-permute-start | bytes 313352 | tf_op jit(solution)/shard_map/ppermute | solution.py:28
  52.2 10.5 %collective-permute-start = (bf16[17,3072]{1,0:T(8,128)(2,1)S(1)}, bf16[17,3072]{1,0:T(8,128)(2,1)S(1)}, u32[]{:S(2)}, u32[]{:S(2)}) collective-permute-start(bf16[17,3072]{1,0:T(8,128)(2,1)S(1)} %get-tuple-element.8), channel_id=1, source_target_pairs={{0,2},{2,4},{4,6},{6,8},{8,10},{10,12},{12,14},{14,0},{1,3},{3,5},... | collective-permute-start | bytes 313352 | tf_op jit(solution)/shard_map/ppermute | solution.py:28
  62.7 12.4 %collective-permute-start.1 = (bf16[17,3072]{1,0:T(8,128)(2,1)S(1)}, bf16[17,3072]{1,0:T(8,128)(2,1)S(1)}, u32[]{:S(2)}, u32[]{:S(2)}) collective-permute-start(bf16[17,3072]{1,0:T(8,128)(2,1)S(1)} %get-tuple-element.7), channel_id=1, source_target_pairs={{0,4},{2,6},{4,8},{6,10},{8,12},{10,14},{12,0},{14,2},{1,5},{3,7},... | collective-permute-start | bytes 313352 | tf_op jit(solution)/shard_map/ppermute | solution.py:28
  75.1 10.3 %collective-permute-start.2 = (bf16[17,3072]{1,0:T(8,128)(2,1)S(1)}, bf16[17,3072]{1,0:T(8,128)(2,1)S(1)}, u32[]{:S(2)}, u32[]{:S(2)}) collective-permute-start(bf16[17,3072]{1,0:T(8,128)(2,1)S(1)} %get-tuple-element.6), channel_id=1, source_target_pairs={{0,6},{2,8},{4,10},{6,12},{8,14},{10,0},{12,2},{14,4},{1,7},{3,9},... | collective-permute-start | bytes 313352 | tf_op jit(solution)/shard_map/ppermute | solution.py:28
